TPU v7x, 256 devices: a whole 4x4x8 slice. The times are simulated.
256 devices in a mesh: band: 8 (over y, core), col: 32 (over z, x).
Axes of the slice: x: 4, y: 4, z: 8, core: 2. Of those that a mesh axis runs over, the one named last changes fastest.
Arguments:
- source: bfloat16 [6, 4194304], P(None, ('band', 'col')), may hold values from -6 to 6
- weights: bfloat16 [65536, 128, 128], P(('band', 'col')), may hold values from -0.5 to 0.5
- source_block: int32 [65536], P(('band', 'col')), may hold values from 0 to 127
- owner_device: int32 [65536, 1], P(('band', 'col')), may hold values from 0 to 255, as said below
- target_tile: int32 [65536], P(('band', 'col')), may hold values from 0 to 112, as said below
- cutoff: int32 [512], P(('band', 'col')), may hold values from 1 to 511
Outputs:
- remapped: float32 [6, 512, 7200], P(None, 'band', 'col')
- filtered: float32 [6, 512, 7200], P(None, 'band', 'col')
Inputs may be any that keep to these rules, and one draw needn't show every extreme that they name: `owner_device`: owners are numbered band index times 32 plus col index. A device's blocks go only to owners in its own band or in the bands next to it. Among the 256 blocks of one device at most 6 share an owner; in every device exactly 6 do for some owner of its own band, and exactly 6 for some owner of each band next to its own; every device sends at least 4 blocks to each owner of its own band. `target_tile`: every tile of every owner receives at least one block.
All inputs are finite; a program needn't handle non-finite values.
Results may differ from a plain program's by a relative error of at most 0.0003.
Values sent between devices are 32-bit elements; how exact they have to be, the bound alone decides.
No kernel may reach another device: no remote copies, remote signals or barrier semaphores. Data moves between devices by JAX's collectives and lax.ppermute only.
A program may use at most 64 MiB of HBM per device.

v0:
```python
import jax
import jax.numpy as jnp
from jax import lax
from jax.sharding import PartitionSpec as P

NLON = 7200
KW = 512


TWO_PI = 6.283185307179586


def extended(array, sides, width):
    for axis, dim in sides:
        size, length = (lax.axis_size(axis), array.shape[dim])
        up = [(i, (i + 1) % size) for i in range(size - 1)]
        down = [(j, i) for i, j in up]
        last = lax.slice_in_dim(array, length - width, length, axis=dim)
        leading = lax.slice_in_dim(array, 0, width, axis=dim)
        before = lax.ppermute(last, axis, up)
        after = lax.ppermute(leading, axis, down)
        array = jnp.concatenate([before, array, after], axis=dim)
    return array


def cut_along(array, dim, size):
    lengths = array.shape
    tiles = array.reshape(*lengths[:dim], size, lengths[dim] // size, *lengths[dim + 1 :])
    return jnp.moveaxis(tiles, dim, 0)


def sent_and_summed(array, axis, dim):
    size = lax.axis_size(axis)
    tiles = lax.all_to_all(cut_along(array, dim, size), axis, 0, 0, tiled=True)
    return jnp.sum(tiles, axis=0)


def joined_along(tiles, dim):
    lengths = list(tiles.shape[1:])
    lengths[dim] *= tiles.shape[0]
    return jnp.moveaxis(tiles, 0, dim).reshape(lengths)


def copy_for_each(array, axis):
    size = lax.axis_size(axis)
    return lax.all_to_all(
        jnp.broadcast_to(array[None], (size, *array.shape)), axis, 0, 0, tiled=True
    )


def collect(array, axis, dim):
    return joined_along(copy_for_each(array, axis), dim)


def zonal_table(start_index, length, period, wave_count):
    positions = start_index + lax.broadcasted_iota(jnp.int32, (length, wave_count), 0)
    wave_index = lax.broadcasted_iota(jnp.int32, (length, wave_count), 1)
    phases = positions * wave_index % period
    angles = phases.astype(jnp.float32) * (TWO_PI / period)
    return jnp.concatenate([jnp.cos(angles), jnp.sin(angles)], axis=1)


def spectral_weights(cutoffs, wave_count, period):
    wave_index = lax.broadcasted_iota(jnp.int32, (cutoffs.shape[0], wave_count), 1)
    scaled = jnp.where(wave_index == 0, 1.0, 2.0) / period
    retained = jnp.where(wave_index <= cutoffs[:, None], scaled, 0.0).astype(jnp.float32)
    return jnp.concatenate([retained, retained], axis=1)


def local(source, weights, source_block, owner_device, target_tile, cutoff):
    col_count = lax.axis_size("col")
    levels = source.shape[0]
    block_count = weights.shape[0]
    block_width = weights.shape[1]
    lat_here = cutoff.shape[0]
    lat_band = lat_here * col_count
    longitudes_here = NLON // col_count
    cell_count = lat_band * longitudes_here
    tile_count = (cell_count + block_width - 1) // block_width
    regular = (tile_count + col_count - 1) // col_count
    capacity = regular + max(
        1, (block_count - col_count * regular + 2 * col_count - 1) // (2 * col_count)
    )
    slot_total = 3 * col_count * capacity
    blocks_here = source.reshape(levels, -1, block_width)
    picked = jnp.take(blocks_here, source_block, axis=1)
    partial_value = jnp.einsum("lnb,nbt->nlt", picked, weights, preferred_element_type=jnp.float32)
    tile_rows = jnp.broadcast_to(
        target_tile.astype(jnp.float32)[:, None, None], (block_count, 1, block_width)
    )
    tagged = jnp.concatenate([partial_value, tile_rows], axis=1)
    owners = owner_device[:, 0]
    owner_band = owners // col_count
    owner_col = owners % col_count
    offset = owner_band - lax.axis_index("band") + 1
    row_index = lax.broadcasted_iota(jnp.int32, (block_count, block_count), 0)
    column_index = lax.broadcasted_iota(jnp.int32, (block_count, block_count), 1)
    earlier = (owners[None, :] == owners[:, None]) & (column_index < row_index)
    rank_within = jnp.sum(earlier.astype(jnp.int32), axis=1)
    slot_index = (offset * col_count + owner_col) * capacity + rank_within
    placing = lax.broadcasted_iota(jnp.int32, (slot_total, block_count), 0) == slot_index[None, :]
    outgoing = jnp.dot(
        placing.astype(jnp.float32),
        tagged.reshape(block_count, (levels + 1) * block_width),
        precision=lax.Precision.HIGHEST,
        preferred_element_type=jnp.float32,
    )
    outgoing = outgoing.reshape(3, col_count, capacity, levels + 1, block_width)
    moved = lax.all_to_all(outgoing, "col", split_axis=1, concat_axis=1, tiled=True)
    rimmed = extended(jnp.stack([moved[0], moved[2]]), (("band", 0),), 1)
    received = jnp.stack([rimmed[0], moved[1], rimmed[3]])
    slot_rows = received.reshape(-1, levels + 1, block_width)
    slot_owned = slot_rows[:, levels, 0].astype(jnp.int32)
    slot_data = slot_rows[:, :levels, :].reshape(-1, levels * block_width)
    chooser = (
        lax.broadcasted_iota(jnp.int32, (tile_count, slot_owned.shape[0]), 0) == slot_owned[None, :]
    ).astype(jnp.float32)
    summed = jnp.dot(
        chooser, slot_data, precision=lax.Precision.HIGHEST, preferred_element_type=jnp.float32
    )
    summed = jnp.transpose(summed.reshape(tile_count, levels, block_width), (1, 0, 2)).reshape(
        levels, tile_count * block_width
    )
    remapped = summed[:, :cell_count].reshape(levels, lat_band, longitudes_here)
    retained = spectral_weights(cutoff, KW, NLON)
    local_table = zonal_table(lax.axis_index("col") * longitudes_here, longitudes_here, NLON, KW)
    partial_spectra = jnp.dot(
        remapped.reshape(levels * lat_band, longitudes_here),
        local_table,
        precision=lax.Precision.HIGHEST,
        preferred_element_type=jnp.float32,
    )
    partial_spectra = partial_spectra.reshape(levels, lat_band, 2 * KW)
    spectrum = sent_and_summed(partial_spectra, "col", 1)
    spectrum = spectrum * retained[None]
    band_spectra = collect(spectrum, "col", 1)
    filtered = jnp.dot(
        band_spectra.reshape(levels * lat_band, 2 * KW),
        local_table.T,
        precision=lax.Precision.HIGHEST,
        preferred_element_type=jnp.float32,
    )
    filtered = filtered.reshape(levels, lat_band, longitudes_here)
    return (remapped, filtered)


def solution(mesh):
    in_specs = (
        P(None, ("band", "col")),
        P(("band", "col"), None, None),
        P(("band", "col")),
        P(("band", "col"), None),
        P(("band", "col")),
        P(("band", "col")),
    )
    out_specs = (P(None, "band", "col"), P(None, "band", "col"))
    return jax.shard_map(local, mesh=mesh, in_specs=in_specs, out_specs=out_specs, check_vma=False)
```

profile of v0, /device:TPU:8, one launch (start us, length us, event | category | flops | bytes accessed | tf_op | source)
XLA Modules:
  0.0 212.5 jit_solution(10348539314015491514)
XLA Ops:
  0.6 0.0 copy-start
  0.6 0.7 compare_select_fusion.1
  1.4 0.7 compare_and_fusion
  2.1 0.9 convert_reduce_fusion
  3.0 0.7 convert_element_type.22
  3.7 0.0 copy-done
  3.7 0.8 gather_fusion
  4.5 4.7 %fusion.12 = f32[256,6,128]{2,1,0:T(8,128)S(1)} fusion(bf16[256,128,128]{2,1,0:T(8,128)(2,1)} %param.7, bf16[256,6,128]{2,1,0:T(8,128)(2,1)S(1)} %gather_fusion, pred[256]{0:T(512)(128)(4,1)S(1)} %compare_and_fusion), kind=kOutput, calls=%fused_computation.17 | convolution fusion | flops 50528256 | bytes 9568512 | tf_op jit(solution)/shard_map/lnb,nbt->nlt/dot_general | solution.py:87
  9.3 0.3 broadcast_in_dim.43
  9.6 0.2 pad_maximum_fusion.1
  9.8 0.4 copy.34
  10.2 0.0 copy-done.3
  10.2 1.2 fusion.8
  11.4 1.2 copy.35
  12.6 68.8 %all_to_all.15 = f32[3,32,6,7,128]{4,3,2,0,1:T(8,128)S(1)} all-to-all(f32[3,32,6,7,128]{4,3,2,0,1:T(8,128)S(1)} %copy.35), channel_id=1, replica_groups=mesh['band'=8,'col'=32] {'col'}, dimensions={1} | all-to-all | bytes 4128768 | tf_op jit(solution)/shard_map/all_to_all | solution.py:109
  81.5 0.2 fusion.37
  81.6 0.2 copy.36
  81.8 1.9 collective-permute-start
  83.8 1.1 copy.37
  84.8 3.8 %collective-permute-start.1 = (f32[1,32,6,7,128]{4,1,3,2,0:T(8,128)}, f32[1,32,6,7,128]{4,1,3,2,0:T(8,128)}, u32[]{:S(2)}, u32[]{:S(2)}) collective-permute-start(f32[1,32,6,7,128]{4,1,3,2,0:T(8,128)} %copy.37), channel_id=1, source_target_pairs={{32,0},{64,32},{96,64},{128,96},{160,128},{192,160},{224,192},{33,... | collective-permute-start | bytes 2064392 | tf_op jit(solution)/shard_map/ppermute | solution.py:21
  88.7 2.0 fusion.21
  90.7 0.0 copy-start.1
  90.7 0.0 copy-start.2
  90.7 3.4 %collective-permute-done = f32[1,32,6,7,128]{4,1,3,2,0:T(8,128)S(1)} collective-permute-done((f32[1,32,6,7,128]{4,1,3,2,0:T(8,128)S(1)}, f32[1,32,6,7,128]{4,1,3,2,0:T(8,128)S(1)}, u32[]{:S(2)}, u32[]{:S(2)}) %collective-permute-start) | collective-permute-done | bytes 688160 | tf_op jit(solution)/shard_map/ppermute | solution.py:20
  94.1 0.4 copy.38
  94.5 2.7 %collective-permute-done.1 = f32[1,32,6,7,128]{4,1,3,2,0:T(8,128)} collective-permute-done((f32[1,32,6,7,128]{4,1,3,2,0:T(8,128)}, f32[1,32,6,7,128]{4,1,3,2,0:T(8,128)}, u32[]{:S(2)}, u32[]{:S(2)}) %collective-permute-start.1) | collective-permute-done | bytes 688160 | tf_op jit(solution)/shard_map/ppermute | solution.py:21
  97.2 1.5 copy.39
  98.7 0.2 pad_maximum_fusion
  98.9 0.2 copy.40
  99.2 0.2 slice_bitcast_fusion
  99.3 10.3 %fusion.24 = s32[576]{0:T(1024)S(1)} fusion(f32[576,7,128]{2,1,0:T(8,128)S(1)} %bitcast.54), kind=kLoop, calls=%fused_computation.32 | loop fusion | flops 576 | bytes 4608 | tf_op jit(solution)/shard_map/convert_element_type | solution.py:113
  109.6 1.0 fusion.2
  110.7 0.1 copy.60
  110.8 0.8 dot_general.34
  111.6 1.4 convolution_bitcast_fusion
  113.0 2.4 %copy.44 = f32[32,6,2,1024]{3,2,1,0:T(2,128)} copy(f32[32,6,2,1024]{3,0,2,1:T(8,128)S(1)} %convolution_bitcast_fusion) | data formatting | bytes 3145728 | tf_op jit(solution)/shard_map/transpose | solution.py:29
  115.4 4.1 %all-to-all-start.1 = ((f32[32,6,2,1024]{3,2,1,0:T(2,128)}), f32[32,6,2,1024]{3,2,1,0:T(2,128)S(1)}, u32[]{:S(2)}, u32[]{:S(2)}) async-start(f32[32,6,2,1024]{3,2,1,0:T(2,128)} %copy.44), calls=%async_computation.1 | async-start | bytes 3145728 | tf_op jit(solution)/shard_map/all_to_all | solution.py:34
  119.6 0.0 copy-done.4
  119.6 0.1 compare_select_fusion
  119.7 39.6 %all-to-all-done.1 = f32[32,6,2,1024]{3,2,1,0:T(2,128)S(1)} async-done(((f32[32,6,2,1024]{3,2,1,0:T(2,128)}), f32[32,6,2,1024]{3,2,1,0:T(2,128)S(1)}, u32[]{:S(2)}, u32[]{:S(2)}) %all-to-all-start.1) | async-done | bytes 1572896 | tf_op jit(solution)/shard_map/all_to_all | solution.py:34
  159.3 0.5 reduce_sum.19
  159.8 1.9 broadcast_in_dim.47
  161.7 5.8 %all-to-all-start.2 = ((f32[32,6,2,1024]{3,2,1,0:T(2,128)}), f32[32,6,2,1024]{3,2,1,0:T(2,128)S(1)}, u32[]{:S(2)}, u32[]{:S(2)}) async-start(f32[32,6,2,1024]{3,2,1,0:T(2,128)} %broadcast_in_dim.47), calls=%async_computation.2 | async-start | bytes 3145728 | tf_op jit(solution)/shard_map/all_to_all | solution.py:46
  167.5 1.2 reshape.134
  168.7 38.7 %all-to-all-done.2 = f32[32,6,2,1024]{3,2,1,0:T(2,128)S(1)} async-done(((f32[32,6,2,1024]{3,2,1,0:T(2,128)}), f32[32,6,2,1024]{3,2,1,0:T(2,128)S(1)}, u32[]{:S(2)}, u32[]{:S(2)}) %all-to-all-start.2) | async-done | bytes 1572896 | tf_op jit(solution)/shard_map/all_to_all | solution.py:46
  207.4 0.6 copy.45
  208.0 1.1 dot_general.36
  209.1 3.3 %fusion.6 = f32[6,64,225]{2,1,0:T(8,128)} fusion(f32[6,64,1024]{2,1,0:T(8,128)S(1)} %dot_general.36, f32[225,512]{1,0:T(8,128)} %copy-done.2, f32[225,512]{1,0:T(8,128)} %copy-done.1), kind=kOutput, calls=%fused_computation.10 | convolution fusion | flops 1061913600 | bytes 2840064 | tf_op jit(solution)/shard_map/dot_general | solution.py:137
  (11 shorter events, 0.1 us)
Async XLA Ops:
  0.6 3.1 %copy-start = (bf16[6,16384]{1,0:T(8,128)(2,1)S(1)}, bf16[6,16384]{1,0:T(8,128)(2,1)}, u32[]{:S(2)}) copy-start(bf16[6,16384]{1,0:T(8,128)(2,1)} %param.6) | copy-start | bytes 589828
  9.3 0.9 copy-start.3
  81.8 12.3 %collective-permute-start = (f32[1,32,6,7,128]{4,1,3,2,0:T(8,128)S(1)}, f32[1,32,6,7,128]{4,1,3,2,0:T(8,128)S(1)}, u32[]{:S(2)}, u32[]{:S(2)}) collective-permute-start(f32[1,32,6,7,128]{4,1,3,2,0:T(8,128)S(1)} %copy.36), channel_id=1, source_target_pairs={{0,32},{32,64},{64,96},{96,128},{128,160},{160,192},{192,224},{1,3... | collective-permute-start | bytes 2064392 | tf_op jit(solution)/shard_map/ppermute | solution.py:20
  84.8 12.4 %collective-permute-start.1 = (f32[1,32,6,7,128]{4,1,3,2,0:T(8,128)}, f32[1,32,6,7,128]{4,1,3,2,0:T(8,128)}, u32[]{:S(2)}, u32[]{:S(2)}) collective-permute-start(f32[1,32,6,7,128]{4,1,3,2,0:T(8,128)} %copy.37), channel_id=1, source_target_pairs={{32,0},{64,32},{96,64},{128,96},{160,128},{192,160},{224,192},{33,... | collective-permute-start | bytes 2064392 | tf_op jit(solution)/shard_map/ppermute | solution.py:21
  90.7 20.9 %copy-start.1 = (f32[225,512]{1,0:T(8,128)}, f32[225,512]{1,0:T(8,128)S(1)}, u32[]{:S(2)}) copy-start(f32[225,512]{1,0:T(8,128)S(1)} %get-tuple-element.5) | copy-start | bytes 1382404
  90.7 20.9 %copy-start.2 = (f32[225,512]{1,0:T(8,128)}, f32[225,512]{1,0:T(8,128)S(1)}, u32[]{:S(2)}) copy-start(f32[225,512]{1,0:T(8,128)S(1)} %get-tuple-element.6) | copy-start | bytes 1382404
  115.4 4.2 %copy-start.4 = (s32[2]{0:T(128)S(1)}, s32[2]{0:T(128)}, u32[]{:S(2)}) copy-start(s32[2]{0:T(128)} %param.11) | copy-start | bytes 28
  115.4 43.8 %all-to-all-start.1 = ((f32[32,6,2,1024]{3,2,1,0:T(2,128)}), f32[32,6,2,1024]{3,2,1,0:T(2,128)S(1)}, u32[]{:S(2)}, u32[]{:S(2)}) async-start(f32[32,6,2,1024]{3,2,1,0:T(2,128)} %copy.44), calls=%async_computation.1 | async-start | bytes 3145728 | tf_op jit(solution)/shard_map/all_to_all | solution.py:34
  161.7 45.7 %all-to-all-start.2 = ((f32[32,6,2,1024]{3,2,1,0:T(2,128)}), f32[32,6,2,1024]{3,2,1,0:T(2,128)S(1)}, u32[]{:S(2)}, u32[]{:S(2)}) async-start(f32[32,6,2,1024]{3,2,1,0:T(2,128)} %broadcast_in_dim.47), calls=%async_computation.2 | async-start | bytes 3145728 | tf_op jit(solution)/shard_map/all_to_all | solution.py:46
where the time goes:
time: 213 us; the launch traced here: 212 us
  waiting for transfers between devices  84.4 us (40%)
  blocking collectives  68.8 us (32%)
  other arithmetic  16.4 us (8%)
  starting transfers between devices  15.7 us (7%)
  local copies, waits for them, and re-layouts  14.6 us (7%)
  matrix products  11.7 us (5%)
    all_to_all x1, blocking collectives, local(): lax.all_to_all(outgoing, 'col', split_axis=1, concat_axis=1, tiled=True)  68.8 us
    all_to_all x1, waiting for transfers between devices, sent_and_summed(): tiles = lax.all_to_all(cut_along(array, dim, size), axis, 0, 0, tiled=True)  39.6 us
    all_to_all x1, waiting for transfers between devices, copy_for_each(): lax.all_to_all(jnp.broadcast_to(array[None], (size, *array.shape)), axis,...  38.7 us
    convert_element_type x1, other arithmetic, local(): slot_owned = slot_rows[:, levels, 0].astype(jnp.int32)  10.3 us
    all_to_all x1, starting transfers between devices, copy_for_each(): lax.all_to_all(jnp.broadcast_to(array[None], (size, *array.shape)), axis,...  5.8 us
    dot_general x1, matrix products, local(): jnp.einsum('lnb,nbt->nlt', picked, weights, preferred_element_type=jnp.fl...  4.73 us
  transfers between devices with their start and end apart: 4, of which 4 were waited for; matrix products, arithmetic and copies ran while one was open for 2% of the time, Pallas kernels for 0%

commit v1 on v0

v1 whole, which is shorter than its diff:
```python
import jax
import jax.numpy as jnp
from jax import lax
from jax.experimental import pallas as pl
from jax.experimental.pallas import tpu as pltpu
from jax.sharding import PartitionSpec as P

NLON = 7200
KW = 512
TWO_PI = 6.283185307179586

LEV = 6
BLK = 128
COLS = 32
LON = NLON // COLS
LATB = 64
CAP = 6
REG = 4
REG_ROWS = REG * LEV
OWN_ROWS = 16
NEAR_ROWS = 40
IRR_ROWS = 88
ID_ROW = 84
TILES = 128
P2_ROWS = 24
OWN_ID = (CAP - REG) * LEV
UP_LANE = REG * LEV
DOWN_LANE = UP_LANE + CAP * LEV
OWN_LANE = DOWN_LANE + CAP * LEV
CHUNK = 64
CHUNKS = 4
AXES = True


def split2(x):
    hi = x.astype(jnp.bfloat16)
    lo = (x - hi.astype(jnp.float32)).astype(jnp.bfloat16)
    return hi, lo


def dot32(a, b):
    return jnp.dot(a, b, preferred_element_type=jnp.float32)


def dot3(a, b):
    return dot32(a[0], b[0]) + (dot32(a[0], b[1]) + dot32(a[1], b[0]))


def place_kernel(sb_hbm, owner_hbm, tile_hbm, src_hbm, w_hbm, reg_hbm, own_hbm, up_hbm, down_hbm, w, src, sb, owners, tiles, buf, marks, count, w_sem, in_sem, out_sem):
    def chunk_copy(i):
        part = pl.ds(i * CHUNK, CHUNK)
        return pltpu.make_async_copy(w_hbm.at[part], w.at[part], w_sem.at[i])

    small = [
        pltpu.make_async_copy(owner_hbm, owners, in_sem.at[0]),
        pltpu.make_async_copy(sb_hbm, sb, in_sem.at[1]),
        pltpu.make_async_copy(tile_hbm, tiles, in_sem.at[2]),
        pltpu.make_async_copy(src_hbm, src, in_sem.at[3]),
    ]
    for copy in small:
        copy.start()
    for i in range(CHUNKS):
        chunk_copy(i).start()
    for i in range(3 * COLS):
        count[i] = 0
    buf[...] = jnp.zeros_like(buf)
    marks[...] = jnp.zeros_like(marks)
    for copy in small:
        copy.wait()
    lane = lax.broadcasted_iota(jnp.int32, (1, BLK), 1)
    first = ((lax.axis_index("band").astype(jnp.int32) if AXES else 3) - 1) * COLS

    def chunk(i, carry):
        chunk_copy(i).wait()
        for u in range(CHUNK):
            n = i * CHUNK + u
            key = owners[n] - first
            start = pl.multiple_of(sb[n] * BLK, BLK)
            value = dot32(src[:, pl.ds(start, BLK)], w[n])
            row = count[key]
            count[key] = row + LEV
            buf[key, pl.ds(row, LEV), :] = value
            at = lane - row
            mark = jnp.where((at >= 0) & (at < LEV), at * TILES + (tiles[n] + 1), 0)
            marks[pl.ds(key, 1), :] = marks[pl.ds(key, 1), :] + mark.astype(jnp.float32)
        return carry

    lax.fori_loop(0, CHUNKS, chunk, 0)
    near = pl.ds(0, COLS)
    own = pl.ds(COLS, COLS)
    below, mine, above = marks[:COLS, :], marks[COLS : 2 * COLS, :], marks[2 * COLS :, :]
    mine = jnp.where(lane < REG_ROWS, mine, 0.0) + jnp.where(
        lane >= OWN_LANE, pltpu.roll(mine, OWN_LANE - REG_ROWS, 1), 0.0
    )
    marks[:COLS, :] = pltpu.roll(below, DOWN_LANE, 1)
    marks[COLS : 2 * COLS, :] = mine
    marks[2 * COLS :, :] = pltpu.roll(above, UP_LANE, 1)
    for key in range(3 * COLS):
        buf[key, CAP * LEV : CAP * LEV + 1, :] = marks[key : key + 1, :]
    parts = (
        (buf.at[pl.ds(2 * COLS, COLS)], up_hbm),
        (buf.at[near], down_hbm),
        (buf.at[own, pl.ds(0, REG_ROWS)], reg_hbm),
        (buf.at[own, pl.ds(REG_ROWS, OWN_ROWS)], own_hbm),
    )
    copies = [pltpu.make_async_copy(part, ref, out_sem.at[i]) for i, (part, ref) in enumerate(parts)]
    for copy in copies:
        copy.start()
    for copy in copies:
        copy.wait()


def place(source, weights, source_block, owners, target_tile, interpret=False):
    hbm = pl.BlockSpec(memory_space=pltpu.HBM)
    blocks = weights.shape[0]
    kinds = (REG_ROWS, OWN_ROWS, NEAR_ROWS, NEAR_ROWS)
    return pl.pallas_call(
        place_kernel,
        out_shape=[jax.ShapeDtypeStruct((COLS, r, BLK), jnp.float32) for r in kinds],
        in_specs=[hbm] * 5,
        out_specs=[hbm] * 4,
        scratch_shapes=[
            pltpu.VMEM(weights.shape, weights.dtype),
            pltpu.VMEM(source.shape, source.dtype),
            pltpu.SMEM((blocks,), jnp.int32),
            pltpu.SMEM((blocks,), jnp.int32),
            pltpu.SMEM((blocks,), jnp.int32),
            pltpu.VMEM((3 * COLS, NEAR_ROWS, BLK), jnp.float32),
            pltpu.VMEM((3 * COLS, BLK), jnp.float32),
            pltpu.SMEM((3 * COLS,), jnp.int32),
            pltpu.SemaphoreType.DMA((CHUNKS,)),
            pltpu.SemaphoreType.DMA((4,)),
            pltpu.SemaphoreType.DMA((4,)),
        ],
        compiler_params=pltpu.CompilerParams(vmem_limit_bytes=58 << 20),
        cost_estimate=pl.CostEstimate(flops=100_000_000, bytes_accessed=10_000_000, transcendentals=0),
        interpret=interpret,
        name="place",
    )(source_block, owners, target_tile, source, weights)


def join_kernel(own_ref, below_ref, above_ref, irr_ref):
    near = CAP * LEV
    for c in range(COLS):
        irr_ref[c, :near, :] = below_ref[c, :near, :]
        irr_ref[c, near : 2 * near, :] = above_ref[c, :near, :]
        irr_ref[c, 2 * near :, :] = own_ref[c]
        ids = own_ref[c, OWN_ID : OWN_ID + 1, :] + below_ref[c, near : near + 1, :] + above_ref[c, near : near + 1, :]
        irr_ref[c, ID_ROW : ID_ROW + 1, :] = ids


def join(own, below, above, interpret=False):
    return pl.pallas_call(
        join_kernel,
        out_shape=jax.ShapeDtypeStruct((COLS, IRR_ROWS, BLK), jnp.float32),
        cost_estimate=pl.CostEstimate(flops=1_000_000, bytes_accessed=3_000_000, transcendentals=0),
        compiler_params=pltpu.CompilerParams(vmem_limit_bytes=12 << 20),
        interpret=interpret,
        name="join",
    )(own, below, above)


def combine_kernel(reg_ref, irr_ref, out_ref, acc, sums):
    rows = lax.broadcasted_iota(jnp.int32, (LEV * TILES, 2 * BLK), 0).astype(jnp.float32) + 1.0
    pad = jnp.zeros((BLK - REG_ROWS - IRR_ROWS, BLK), jnp.float32)
    for s in range(0, COLS, 2):
        data = jnp.concatenate([reg_ref[s], irr_ref[s], pad, reg_ref[s + 1], irr_ref[s + 1], pad], axis=0)
        ids = jnp.concatenate([irr_ref[s, ID_ROW : ID_ROW + 1, :], irr_ref[s + 1, ID_ROW : ID_ROW + 1, :]], axis=1)
        chooser = jnp.where(rows == ids, 1.0, 0.0).astype(jnp.bfloat16)
        both = jnp.concatenate(split2(data), axis=1)
        part = dot32(chooser, both)
        if s == 0:
            acc[...] = part
        else:
            acc[...] += part
    sums[...] = acc[:, :BLK] + acc[:, BLK:]
    lane = lax.broadcasted_iota(jnp.int32, (LEV, BLK), 1)
    for lat in range(LATB):
        for half in range(2):
            first, shift = divmod(lat * LON + half * BLK, BLK)
            value = sums[pl.ds(first, LEV, stride=TILES), :]
            if shift:
                later = sums[pl.ds(first + 1, LEV, stride=TILES), :]
                value = jnp.where(lane < BLK - shift, pltpu.roll(value, BLK - shift, 1), pltpu.roll(later, BLK - shift, 1))
            at = (lat % 2) * 2 * LEV + half * LEV
            out_ref[lat // 2, at : at + LEV, :] = value


def combine(reg, irr, interpret=False):
    return pl.pallas_call(
        combine_kernel,
        out_shape=jax.ShapeDtypeStruct((COLS, P2_ROWS, BLK), jnp.float32),
        scratch_shapes=[
            pltpu.VMEM((LEV * TILES, 2 * BLK), jnp.float32),
            pltpu.VMEM((LEV * TILES, BLK), jnp.float32),
        ],
        compiler_params=pltpu.CompilerParams(vmem_limit_bytes=24 << 20),
        cost_estimate=pl.CostEstimate(flops=1_600_000_000, bytes_accessed=2_000_000, transcendentals=0),
        interpret=interpret,
        name="combine",
    )(reg, irr)


def filter_kernel(cut_ref, x_ref, f_ref, ft_ref, g_ref, gt_ref, tc_ref, ts_ref, out_ref):
    lat_count = 2
    pieces = []
    for p in range(lat_count):
        for l in range(LEV):
            for h in range(2):
                pieces.append(x_ref[pl.ds(p * 2 * LEV + h * LEV + l, COLS, stride=P2_ROWS), :])
    x = jnp.concatenate(pieces, axis=1)
    f = (f_ref[0], f_ref[1])
    ft = (ft_ref[0], ft_ref[1])
    g = (g_ref[0], g_ref[1])
    gt = (gt_ref[0], gt_ref[1])
    tc, ts = tc_ref[...], ts_ref[...]
    y = dot3(f, split2(x))
    rows = []
    for r in range(lat_count * LEV):
        re, im = y[:COLS, r * 256 : r * 256 + 256], y[COLS:, r * 256 : r * 256 + 256]
        rows.append(jnp.concatenate([re * tc + im * ts, im * tc - re * ts], axis=1))
    u = jnp.concatenate(rows, axis=0)
    z = dot3(split2(u), g)
    row = lax.broadcasted_iota(jnp.int32, z.shape, 0)
    m = lax.broadcasted_iota(jnp.int32, z.shape, 1) % (KW // COLS)
    k = row % COLS + COLS * m
    cut = jnp.where(row < LEV * COLS, cut_ref[0], cut_ref[1])
    gain = jnp.where(k == 0, 1.0 / NLON, 2.0 / NLON)
    z = z * jnp.where(k <= cut, gain, 0.0)
    w = dot3(split2(z), gt)
    cols = []
    for r in range(lat_count * LEV):
        part = w[r * COLS : r * COLS + COLS]
        re, im = part[:, :256], part[:, 256:]
        cols.append(jnp.concatenate([re * tc - im * ts, re * ts + im * tc], axis=0))
    v = jnp.concatenate(cols, axis=1)
    out = dot3(ft, split2(v))
    at = 0
    for p in range(lat_count):
        for l in range(LEV):
            for h in range(2):
                out_ref[pl.ds(p * 2 * LEV + h * LEV + l, COLS, stride=P2_ROWS), :] = out[:, at * BLK : at * BLK + BLK]
                at += 1


def zonal_filter(rows, cutoff, tables, interpret=False):
    vmem = pl.BlockSpec(memory_space=pltpu.VMEM)
    out = pl.pallas_call(
        filter_kernel,
        out_shape=jax.ShapeDtypeStruct((COLS * P2_ROWS, BLK), jnp.float32),
        in_specs=[pl.BlockSpec(memory_space=pltpu.SMEM)] + [vmem] * 7,
        out_specs=vmem,
        compiler_params=pltpu.CompilerParams(vmem_limit_bytes=24 << 20),
        cost_estimate=pl.CostEstimate(flops=300_000_000, bytes_accessed=1_000_000, transcendentals=0),
        interpret=interpret,
        name="zonal",
    )(cutoff, rows.reshape(COLS * P2_ROWS, BLK), *tables)
    return out.reshape(COLS, P2_ROWS, BLK)


def angles(shape, factor, period):
    a = lax.broadcasted_iota(jnp.int32, shape, 0)
    b = lax.broadcasted_iota(jnp.int32, shape, 1)
    phases = a * b * factor % period
    return phases.astype(jnp.float32) * (TWO_PI / period)


def stack2(x):
    hi = lax.reduce_precision(x, 8, 7)
    return jnp.stack([hi.astype(jnp.bfloat16), (x - hi).astype(jnp.bfloat16)])


def zonal_tables():
    theta = angles((COLS, COLS), 1, COLS)
    f = jnp.concatenate([jnp.cos(theta), -jnp.sin(theta)], axis=0)
    turn = angles((COLS, 256), 1, NLON)
    tc, ts = jnp.cos(turn), jnp.sin(turn)
    phi = angles((KW // COLS, 256), COLS, NLON)
    inside = lax.broadcasted_iota(jnp.int32, phi.shape, 1) < LON
    c, s = jnp.where(inside, jnp.cos(phi), 0.0), jnp.where(inside, jnp.sin(phi), 0.0)
    gt = jnp.concatenate([jnp.concatenate([c, s], axis=1), jnp.concatenate([-s, c], axis=1)], axis=0)
    return stack2(f), stack2(f.T), stack2(gt.T), stack2(gt), tc, ts


def lay_kernel(rows_ref, out_ref, low, high):
    for h, half in enumerate((low, high)):
        for p in range(2):
            for l in range(LEV):
                part = rows_ref[pl.ds(p * 2 * LEV + h * LEV + l, COLS, stride=P2_ROWS), :]
                half[pl.ds(l * LATB + p, COLS, stride=2), :] = part
    for l in range(LEV):
        out_ref[l, :, :BLK] = low[l * LATB : l * LATB + LATB, :]
        out_ref[l, :, BLK:] = high[l * LATB : l * LATB + LATB, : LON - BLK]


def by_latitude(rows, interpret=False):
    return pl.pallas_call(
        lay_kernel,
        out_shape=jax.ShapeDtypeStruct((LEV, LATB, LON), jnp.float32),
        scratch_shapes=[pltpu.VMEM((LEV * LATB, BLK), jnp.float32)] * 2,
        cost_estimate=pl.CostEstimate(flops=1_000_000, bytes_accessed=800_000, transcendentals=0),
        compiler_params=pltpu.CompilerParams(vmem_limit_bytes=8 << 20),
        interpret=interpret,
        name="lay",
    )(rows.reshape(COLS * P2_ROWS, BLK))


def exchange(array):
    return lax.all_to_all(array, "col", 0, 0, tiled=True)


def local(source, weights, source_block, owner_device, target_tile, cutoff):
    bands = lax.axis_size("band")
    reg, own, up, down = place(source, weights, source_block, owner_device[:, 0], target_tile)
    steps = [(i, i + 1) for i in range(bands - 1)]
    below = lax.ppermute(up, "band", steps)
    above = lax.ppermute(down, "band", [(j, i) for i, j in steps])
    reg = exchange(reg)
    irr = exchange(join(own, below, above))
    rows = combine(reg, irr)
    remapped = by_latitude(rows)
    rows = exchange(rows)
    rows = zonal_filter(rows, cutoff, zonal_tables())
    filtered = by_latitude(exchange(rows))
    return (remapped, filtered)


def solution(mesh):
    in_specs = (
        P(None, ("band", "col")),
        P(("band", "col"), None, None),
        P(("band", "col")),
        P(("band", "col"), None),
        P(("band", "col")),
        P(("band", "col")),
    )
    out_specs = (P(None, "band", "col"), P(None, "band", "col"))
    return jax.shard_map(local, mesh=mesh, in_specs=in_specs, out_specs=out_specs, check_vma=False)
```

time: 213 us -> 130 us (0.61)
  blocking collectives: 68.8 us -> 0 us
  starting transfers between devices: 15.7 us -> 36.6 us
  Pallas kernels: 0 us -> 17.1 us
  other arithmetic: 16.4 us -> 0.65 us
  local copies, waits for them, and re-layouts: 14.6 us -> 1.23 us
  matrix products: 11.7 us -> 0 us
  waiting for transfers between devices: 84.4 us -> 73.3 us
    all_to_all x1 -> x0, blocking collectives: 68.8 us -> none  [local(): lax.all_to_all(outgoing, 'col', split_axis=1, concat_axis=1, tiled=True)]
    all_to_all x2 -> x4, starting transfers between devices: 9.94 us -> 31 us  [exchange(): return lax.all_to_all(array, 'col', 0, 0, tiled=True)]
    pallas_call x0 -> x6, Pallas kernels: none -> 17.1 us  [the longest x1 6.99 us: place(): pl.pallas_call(place_kernel, out_shape=[jax.ShapeDtypeStruct((COLS, r, BL...]
    all_to_all x2 -> x4, waiting for transfers between devices: 78.3 us -> 64.9 us  [exchange(): return lax.all_to_all(array, 'col', 0, 0, tiled=True)]
    dot_general x5 -> x0, matrix products: 11.7 us -> none  [the longest x1 4.73 us: local(): jnp.einsum('lnb,nbt->nlt', picked, weights, preferred_element_type=jnp.fl...]
    convert_element_type x2, other arithmetic: 11 us -> 0.09 us  [stack2(): return jnp.stack([hi.astype(jnp.bfloat16), (x - hi).astype(jnp.bfloat16)])]
    dot_general x4 -> x0, local copies, waits for them, and re-layouts: 3.26 us -> none  [the longest x1 1.22 us: local(): jnp.dot(placing.astype(jnp.float32), tagged.reshape(block_count, (levels...]
    transpose x2 -> x0, local copies, waits for them, and re-layouts: 3.03 us -> none  [the longest x1 2.38 us: cut_along(): return jnp.moveaxis(tiles, dim, 0)]
  transfers between devices with their start and end apart: 4 -> 6, of which waited for: 4 -> 5; matrix products, arithmetic and copies ran while one was open for 2% -> 1% of each run, Pallas kernels for 0% -> 2%
where the time goes in v1:
time: 130 us
  waiting for transfers between devices  73.3 us (56%)
  starting transfers between devices  36.6 us (28%)
  Pallas kernels  17.1 us (13%)
    all_to_all x4, waiting for transfers between devices, exchange(): return lax.all_to_all(array, 'col', 0, 0, tiled=True)  64.9 us
    all_to_all x4, starting transfers between devices, exchange(): return lax.all_to_all(array, 'col', 0, 0, tiled=True)  31 us
    pallas_call x1, Pallas kernels, place(): pl.pallas_call(place_kernel, out_shape=[jax.ShapeDtypeStruct((COLS, r, BL...  6.99 us
    ppermute x1, waiting for transfers between devices, local(): below = lax.ppermute(up, 'band', steps)  6.54 us
    ppermute x1, starting transfers between devices, local(): above = lax.ppermute(down, 'band', [(j, i) for i, j in steps])  3.64 us
    pallas_call x1, Pallas kernels, zonal_filter(): pl.pallas_call(filter_kernel, out_shape=jax.ShapeDtypeStruct((COLS * P2_R...  3.34 us
    pallas_call x1, Pallas kernels, combine(): pl.pallas_call(combine_kernel, out_shape=jax.ShapeDtypeStruct((COLS, P2_R...  2.85 us
    pallas_call x2, Pallas kernels, by_latitude(): pl.pallas_call(lay_kernel, out_shape=jax.ShapeDtypeStruct((LEV, LATB, LON...  2.69 us
  transfers between devices with their start and end apart: 6, of which 5 were waited for; matrix products, arithmetic and copies ran while one was open for 1% of the time, Pallas kernels for 2%

profile of v1, /device:TPU:8, one launch (start us, length us, event | category | flops | bytes accessed | tf_op | source)
XLA Modules:
  0.0 129.6 jit_solution(18012853879902058381)
XLA Ops:
  0.6 7.0 %place.1 = (f32[32,24,128]{2,1,0:T(8,128)}, f32[32,16,128]{2,1,0:T(8,128)}, f32[32,40,128]{2,1,0:T(8,128)}, f32[32,40,128]{2,1,0:T(8,128)}) custom-call(s32[256]{0:T(256)} %sb_hbm.1, s32[256]{0:T(256)} %bitcast.39, s32[256]{0:T(256)} %tile_hbm.1, bf16[6,16384]{1,0:T(8,128)(2,1)} %src_hbm.1, bf16[256,128,128]{2,1,0:T(8,128)(2,1)} %w_hbm.1), custom_call_target="tpu_custom_call" | custom-call | flops 100000000 | bytes 10000000 | tf_op jit(solution)/shard_map/place/pallas_call | solution.py:117
  7.6 11.3 %all-to-all-start = ((f32[32,24,128]{2,1,0:T(8,128)}), f32[32,24,128]{2,1,0:T(8,128)S(1)}, u32[]{:S(2)}, u32[]{:S(2)}) async-start(f32[32,24,128]{2,1,0:T(8,128)} %get-tuple-element.6), calls=%async_computation | async-start | bytes 786432 | tf_op jit(solution)/shard_map/all_to_all | solution.py:309
  19.0 1.9 %collective-permute-start = (f32[32,40,128]{2,1,0:T(8,128)}, f32[32,40,128]{2,1,0:T(8,128)S(1)}, u32[]{:S(2)}, u32[]{:S(2)}) collective-permute-start(f32[32,40,128]{2,1,0:T(8,128)} %get-tuple-element.8), channel_id=1, source_target_pairs={{0,32},{32,64},{64,96},{96,128},{128,160},{160,192},{192,224},{1,3... | collective-permute-start | bytes 1966088 | tf_op jit(solution)/shard_map/ppermute | solution.py:316
  20.9 3.6 %collective-permute-start.1 = (f32[32,40,128]{2,1,0:T(8,128)}, f32[32,40,128]{2,1,0:T(8,128)S(1)}, u32[]{:S(2)}, u32[]{:S(2)}) collective-permute-start(f32[32,40,128]{2,1,0:T(8,128)} %get-tuple-element.9), channel_id=1, source_target_pairs={{32,0},{64,32},{96,64},{128,96},{160,128},{192,160},{224,192},{33,... | collective-permute-start | bytes 1966088 | tf_op jit(solution)/shard_map/ppermute | solution.py:317
  24.5 6.5 %collective-permute-done.below_ref = f32[32,40,128]{2,1,0:T(8,128)S(1)} collective-permute-done((f32[32,40,128]{2,1,0:T(8,128)}, f32[32,40,128]{2,1,0:T(8,128)S(1)}, u32[]{:S(2)}, u32[]{:S(2)}) %collective-permute-start) | collective-permute-done | bytes 655392 | tf_op jit(solution)/shard_map/ppermute | solution.py:316
  31.1 1.9 %collective-permute-done.1.above_ref = f32[32,40,128]{2,1,0:T(8,128)S(1)} collective-permute-done((f32[32,40,128]{2,1,0:T(8,128)}, f32[32,40,128]{2,1,0:T(8,128)S(1)}, u32[]{:S(2)}, u32[]{:S(2)}) %collective-permute-start.1) | collective-permute-done | bytes 655392 | tf_op jit(solution)/shard_map/ppermute | solution.py:317
  32.9 0.0 copy-start
  32.9 0.9 copy-done
  33.9 1.2 join.1
  35.1 0.0 all-to-all-done.reg_ref
  35.1 9.8 %all-to-all-start.1 = ((f32[32,88,128]{2,1,0:T(8,128)}), f32[32,88,128]{2,1,0:T(8,128)S(1)}, u32[]{:S(2)}, u32[]{:S(2)}) async-start(f32[32,88,128]{2,1,0:T(8,128)} %join.1), calls=%async_computation.1 | async-start | bytes 2883584 | tf_op jit(solution)/shard_map/all_to_all | solution.py:309
  44.9 0.1 fusion.27
  45.0 0.1 reduce-precision_convert_fusion.3
  45.1 0.1 copy.8.f_ref
  45.2 0.1 sine_select_fusion
  45.3 0.2 copy.9.g_ref
  45.5 0.0 copy-start.1
  45.5 36.5 %all-to-all-done.1.irr_ref = f32[32,88,128]{2,1,0:T(8,128)S(1)} async-done(((f32[32,88,128]{2,1,0:T(8,128)}), f32[32,88,128]{2,1,0:T(8,128)S(1)}, u32[]{:S(2)}, u32[]{:S(2)}) %all-to-all-start.1) | async-done | bytes 1441824 | tf_op jit(solution)/shard_map/all_to_all | solution.py:309
  82.1 2.9 %combine.1 = f32[32,24,128]{2,1,0:T(8,128)} custom-call(f32[32,24,128]{2,1,0:T(8,128)S(1)} %all-to-all-done.reg_ref, f32[32,88,128]{2,1,0:T(8,128)S(1)} %all-to-all-done.1.irr_ref), custom_call_target="tpu_custom_call" | custom-call | flops 1600000000 | bytes 2000000 | tf_op jit(solution)/shard_map/combine/pallas_call | solution.py:190
  84.9 5.7 %all-to-all-start.2 = ((f32[32,24,128]{2,1,0:T(8,128)}), f32[32,24,128]{2,1,0:T(8,128)S(1)}, u32[]{:S(2)}, u32[]{:S(2)}) async-start(f32[32,24,128]{2,1,0:T(8,128)} %combine.1), calls=%async_computation.2 | async-start | bytes 786432 | tf_op jit(solution)/shard_map/all_to_all | solution.py:309
  90.6 0.1 sine_negate_fusion
  90.7 0.1 fusion.25
  90.8 0.2 fusion.7
  91.0 15.6 %all-to-all-done.2 = f32[32,24,128]{2,1,0:T(8,128)S(1)} async-done(((f32[32,24,128]{2,1,0:T(8,128)}), f32[32,24,128]{2,1,0:T(8,128)S(1)}, u32[]{:S(2)}, u32[]{:S(2)}) %all-to-all-start.2) | async-done | bytes 393248 | tf_op jit(solution)/shard_map/all_to_all | solution.py:309
  106.6 0.0 copy-done.1
  106.6 3.3 %zonal.1 = f32[768,128]{1,0:T(8,128)} custom-call(s32[2]{0:T(128)S(1)} %copy-done.1, f32[768,128]{1,0:T(8,128)S(1)} %bitcast.38, bf16[2,64,32]{2,1,0:T(8,128)(2,1)S(1)} %copy.8.f_ref, bf16[2,32,64]{2,1,0:T(8,128)(2,1)S(1)} %pad_maximum_fusion.5.ft_ref, bf16[2,512,32]{2,1,0:T(8,128)(2,1)S(1)} %copy.9.g_ref, bf16[2,32,512]{2,1,0:T(8,128)(2,1)S(1)} %pad_maximum_fusion.2.gt_ref, ...), custom_call_target="tpu_custom_call" | custom-call | flops 300000000 | bytes 1000000 | tf_op jit(solution)/shard_map/zonal/pallas_call | solution.py:248
  110.0 4.2 %all-to-all-start.3 = ((f32[32,24,128]{2,1,0:T(8,128)}), f32[32,24,128]{2,1,0:T(8,128)S(1)}, u32[]{:S(2)}, u32[]{:S(2)}) async-start(f32[32,24,128]{2,1,0:T(8,128)} %bitcast.13), calls=%async_computation.3 | async-start | bytes 786432 | tf_op jit(solution)/shard_map/all_to_all | solution.py:309
  114.2 1.8 %lay.2 = f32[6,64,225]{2,1,0:T(8,128)} custom-call(f32[768,128]{1,0:T(8,128)} %bitcast.1.rows_ref), custom_call_target="tpu_custom_call" | custom-call | flops 1000000 | bytes 800000 | tf_op jit(solution)/shard_map/lay/pallas_call | solution.py:297
  116.0 12.8 %all-to-all-done.3 = f32[32,24,128]{2,1,0:T(8,128)S(1)} async-done(((f32[32,24,128]{2,1,0:T(8,128)}), f32[32,24,128]{2,1,0:T(8,128)S(1)}, u32[]{:S(2)}, u32[]{:S(2)}) %all-to-all-start.3) | async-done | bytes 393248 | tf_op jit(solution)/shard_map/all_to_all | solution.py:309
  128.8 0.8 lay.3
  (8 shorter events, 0.1 us)
Async XLA Ops:
  7.6 27.5 %all-to-all-start = ((f32[32,24,128]{2,1,0:T(8,128)}), f32[32,24,128]{2,1,0:T(8,128)S(1)}, u32[]{:S(2)}, u32[]{:S(2)}) async-start(f32[32,24,128]{2,1,0:T(8,128)} %get-tuple-element.6), calls=%async_computation | async-start | bytes 786432 | tf_op jit(solution)/shard_map/all_to_all | solution.py:309
  19.0 12.1 %collective-permute-start = (f32[32,40,128]{2,1,0:T(8,128)}, f32[32,40,128]{2,1,0:T(8,128)S(1)}, u32[]{:S(2)}, u32[]{:S(2)}) collective-permute-start(f32[32,40,128]{2,1,0:T(8,128)} %get-tuple-element.8), channel_id=1, source_target_pairs={{0,32},{32,64},{64,96},{96,128},{128,160},{160,192},{192,224},{1,3... | collective-permute-start | bytes 1966088 | tf_op jit(solution)/shard_map/ppermute | solution.py:316
  20.9 12.0 %collective-permute-start.1 = (f32[32,40,128]{2,1,0:T(8,128)}, f32[32,40,128]{2,1,0:T(8,128)S(1)}, u32[]{:S(2)}, u32[]{:S(2)}) collective-permute-start(f32[32,40,128]{2,1,0:T(8,128)} %get-tuple-element.9), channel_id=1, source_target_pairs={{32,0},{64,32},{96,64},{128,96},{160,128},{192,160},{224,192},{33,... | collective-permute-start | bytes 1966088 | tf_op jit(solution)/shard_map/ppermute | solution.py:317
  32.9 0.9 copy-start
  35.1 46.9 %all-to-all-start.1 = ((f32[32,88,128]{2,1,0:T(8,128)}), f32[32,88,128]{2,1,0:T(8,128)S(1)}, u32[]{:S(2)}, u32[]{:S(2)}) async-start(f32[32,88,128]{2,1,0:T(8,128)} %join.1), calls=%async_computation.1 | async-start | bytes 2883584 | tf_op jit(solution)/shard_map/all_to_all | solution.py:309
  45.5 61.1 %copy-start.1 = (s32[2]{0:T(128)S(1)}, s32[2]{0:T(128)}, u32[]{:S(2)}) copy-start(s32[2]{0:T(128)} %cut_ref.1) | copy-start | bytes 28
  84.9 21.7 %all-to-all-start.2 = ((f32[32,24,128]{2,1,0:T(8,128)}), f32[32,24,128]{2,1,0:T(8,128)S(1)}, u32[]{:S(2)}, u32[]{:S(2)}) async-start(f32[32,24,128]{2,1,0:T(8,128)} %combine.1), calls=%async_computation.2 | async-start | bytes 786432 | tf_op jit(solution)/shard_map/all_to_all | solution.py:309
  110.0 18.8 %all-to-all-start.3 = ((f32[32,24,128]{2,1,0:T(8,128)}), f32[32,24,128]{2,1,0:T(8,128)S(1)}, u32[]{:S(2)}, u32[]{:S(2)}) async-start(f32[32,24,128]{2,1,0:T(8,128)} %bitcast.13), calls=%async_computation.3 | async-start | bytes 786432 | tf_op jit(solution)/shard_map/all_to_all | solution.py:309

commit v2 on v1

--- a/solution.py
+++ b/solution.py
@@ -15,18 +15,12 @@
 LON = NLON // COLS
 LATB = 64
 CAP = 6
-REG = 4
-REG_ROWS = REG * LEV
-OWN_ROWS = 16
-NEAR_ROWS = 40
-IRR_ROWS = 88
-ID_ROW = 84
-TILES = 128
+SIDE_ROWS = CAP * LEV
+ID_ROW = 3 * SIDE_ROWS
+ROWS = ID_ROW + 4
+WINDOW = 8
+TILES = 120
 P2_ROWS = 24
-OWN_ID = (CAP - REG) * LEV
-UP_LANE = REG * LEV
-DOWN_LANE = UP_LANE + CAP * LEV
-OWN_LANE = DOWN_LANE + CAP * LEV
 CHUNK = 64
 CHUNKS = 4
 AXES = True
@@ -46,7 +40,7 @@
     return dot32(a[0], b[0]) + (dot32(a[0], b[1]) + dot32(a[1], b[0]))
 
 
-def place_kernel(sb_hbm, owner_hbm, tile_hbm, src_hbm, w_hbm, reg_hbm, own_hbm, up_hbm, down_hbm, w, src, sb, owners, tiles, buf, marks, count, w_sem, in_sem, out_sem):
+def place_kernel(sb_hbm, owner_hbm, tile_hbm, src_hbm, w_hbm, out_hbm, w, src, sb, owners, tiles, buf, marks, count, w_sem, in_sem, out_sem):
     def chunk_copy(i):
         part = pl.ds(i * CHUNK, CHUNK)
         return pltpu.make_async_copy(w_hbm.at[part], w.at[part], w_sem.at[i])
@@ -67,8 +61,13 @@
     marks[...] = jnp.zeros_like(marks)
     for copy in small:
         copy.wait()
-    lane = lax.broadcasted_iota(jnp.int32, (1, BLK), 1)
-    first = ((lax.axis_index("band").astype(jnp.int32) if AXES else 3) - 1) * COLS
+    band = lax.axis_index("band").astype(jnp.int32) if AXES else 3
+    col = lax.axis_index("col").astype(jnp.int32) if AXES else 5
+    first = (band - 1) * COLS
+    odd = band % 2
+    side_base = jnp.where(odd == 1, 0, 2 * SIDE_ROWS)
+    side_step = jnp.where(odd == 1, SIDE_ROWS, -SIDE_ROWS)
+    lane = (lax.broadcasted_iota(jnp.int32, (1, BLK), 1) - col % (COLS // 2) * WINDOW) * LEV
 
     def chunk(i, carry):
         chunk_copy(i).wait()
@@ -79,58 +78,43 @@
             value = dot32(src[:, pl.ds(start, BLK)], w[n])
             row = count[key]
             count[key] = row + LEV
-            buf[key, pl.ds(row, LEV), :] = value
-            at = lane - row
-            mark = jnp.where((at >= 0) & (at < LEV), at * TILES + (tiles[n] + 1), 0)
+            buf[key & (COLS - 1), pl.ds((key >> 5) * side_step + (side_base + row), LEV), :] = value
+            mark = jnp.where(lane == row, tiles[n] + 1, 0)
             marks[pl.ds(key, 1), :] = marks[pl.ds(key, 1), :] + mark.astype(jnp.float32)
         return carry
 
     lax.fori_loop(0, CHUNKS, chunk, 0)
-    near = pl.ds(0, COLS)
-    own = pl.ds(COLS, COLS)
-    below, mine, above = marks[:COLS, :], marks[COLS : 2 * COLS, :], marks[2 * COLS :, :]
-    mine = jnp.where(lane < REG_ROWS, mine, 0.0) + jnp.where(
-        lane >= OWN_LANE, pltpu.roll(mine, OWN_LANE - REG_ROWS, 1), 0.0
-    )
-    marks[:COLS, :] = pltpu.roll(below, DOWN_LANE, 1)
-    marks[COLS : 2 * COLS, :] = mine
-    marks[2 * COLS :, :] = pltpu.roll(above, UP_LANE, 1)
+    below, above = marks[:COLS, :], marks[2 * COLS :, :]
+    marks[:COLS, :] = jnp.where(odd == 1, below, above)
+    marks[2 * COLS :, :] = pltpu.roll(jnp.where(odd == 1, above, below), WINDOW - CAP, 1)
     for key in range(3 * COLS):
-        buf[key, CAP * LEV : CAP * LEV + 1, :] = marks[key : key + 1, :]
-    parts = (
-        (buf.at[pl.ds(2 * COLS, COLS)], up_hbm),
-        (buf.at[near], down_hbm),
-        (buf.at[own, pl.ds(0, REG_ROWS)], reg_hbm),
-        (buf.at[own, pl.ds(REG_ROWS, OWN_ROWS)], own_hbm),
-    )
-    copies = [pltpu.make_async_copy(part, ref, out_sem.at[i]) for i, (part, ref) in enumerate(parts)]
-    for copy in copies:
-        copy.start()
-    for copy in copies:
-        copy.wait()
+        row = ID_ROW + key // COLS
+        buf[key % COLS, row : row + 1, :] = marks[key : key + 1, :]
+    out = pltpu.make_async_copy(buf, out_hbm, out_sem)
+    out.start()
+    out.wait()
 
 
 def place(source, weights, source_block, owners, target_tile, interpret=False):
     hbm = pl.BlockSpec(memory_space=pltpu.HBM)
     blocks = weights.shape[0]
-    kinds = (REG_ROWS, OWN_ROWS, NEAR_ROWS, NEAR_ROWS)
     return pl.pallas_call(
         place_kernel,
-        out_shape=[jax.ShapeDtypeStruct((COLS, r, BLK), jnp.float32) for r in kinds],
+        out_shape=jax.ShapeDtypeStruct((COLS, ROWS, BLK), jnp.float32),
         in_specs=[hbm] * 5,
-        out_specs=[hbm] * 4,
+        out_specs=hbm,
         scratch_shapes=[
             pltpu.VMEM(weights.shape, weights.dtype),
             pltpu.VMEM(source.shape, source.dtype),
             pltpu.SMEM((blocks,), jnp.int32),
             pltpu.SMEM((blocks,), jnp.int32),
             pltpu.SMEM((blocks,), jnp.int32),
-            pltpu.VMEM((3 * COLS, NEAR_ROWS, BLK), jnp.float32),
+            pltpu.VMEM((COLS, ROWS, BLK), jnp.float32),
             pltpu.VMEM((3 * COLS, BLK), jnp.float32),
             pltpu.SMEM((3 * COLS,), jnp.int32),
             pltpu.SemaphoreType.DMA((CHUNKS,)),
             pltpu.SemaphoreType.DMA((4,)),
-            pltpu.SemaphoreType.DMA((4,)),
+            pltpu.SemaphoreType.DMA,
         ],
         compiler_params=pltpu.CompilerParams(vmem_limit_bytes=58 << 20),
         cost_estimate=pl.CostEstimate(flops=100_000_000, bytes_accessed=10_000_000, transcendentals=0),
@@ -139,41 +123,35 @@
     )(source_block, owners, target_tile, source, weights)
 
 
-def join_kernel(own_ref, below_ref, above_ref, irr_ref):
-    near = CAP * LEV
-    for c in range(COLS):
-        irr_ref[c, :near, :] = below_ref[c, :near, :]
-        irr_ref[c, near : 2 * near, :] = above_ref[c, :near, :]
-        irr_ref[c, 2 * near :, :] = own_ref[c]
-        ids = own_ref[c, OWN_ID : OWN_ID + 1, :] + below_ref[c, near : near + 1, :] + above_ref[c, near : near + 1, :]
-        irr_ref[c, ID_ROW : ID_ROW + 1, :] = ids
-
-
-def join(own, below, above, interpret=False):
+def sum_side(side, got_ref, out_ref):
+    begin = min(side * CAP, 3 * CAP - WINDOW) * LEV
+    halves = []
+    for half in range(2):
+        at = half * (COLS // 2) * ROWS + ID_ROW + side
+        marks = [got_ref[pl.ds(at + g * 8 * ROWS, 8, stride=ROWS), :] for g in range(2)]
+        halves.append(jnp.sum(marks[0] + marks[1], axis=0, keepdims=True))
+    ids = jnp.concatenate(halves, axis=1)
+    tile = lax.broadcasted_iota(jnp.int32, (TILES, 2 * BLK), 0).astype(jnp.float32) + 1.0
+    chooser = jnp.where(tile == ids, 1.0, 0.0).astype(jnp.bfloat16)
+    for l in range(LEV):
+        data = [got_ref[pl.ds(s * ROWS + begin + l, WINDOW, stride=LEV), :] for s in range(COLS)]
+        both = dot32(chooser, jnp.concatenate(split2(jnp.concatenate(data, axis=0)), axis=1))
+        out_ref[l * TILES : l * TILES + TILES, :] = both[:, :BLK] + both[:, BLK:]
+
+
+def tile_sums(got, side, interpret=False):
     return pl.pallas_call(
-        join_kernel,
-        out_shape=jax.ShapeDtypeStruct((COLS, IRR_ROWS, BLK), jnp.float32),
-        cost_estimate=pl.CostEstimate(flops=1_000_000, bytes_accessed=3_000_000, transcendentals=0),
-        compiler_params=pltpu.CompilerParams(vmem_limit_bytes=12 << 20),
-        interpret=interpret,
-        name="join",
-    )(own, below, above)
-
-
-def combine_kernel(reg_ref, irr_ref, out_ref, acc, sums):
-    rows = lax.broadcasted_iota(jnp.int32, (LEV * TILES, 2 * BLK), 0).astype(jnp.float32) + 1.0
-    pad = jnp.zeros((BLK - REG_ROWS - IRR_ROWS, BLK), jnp.float32)
-    for s in range(0, COLS, 2):
-        data = jnp.concatenate([reg_ref[s], irr_ref[s], pad, reg_ref[s + 1], irr_ref[s + 1], pad], axis=0)
-        ids = jnp.concatenate([irr_ref[s, ID_ROW : ID_ROW + 1, :], irr_ref[s + 1, ID_ROW : ID_ROW + 1, :]], axis=1)
-        chooser = jnp.where(rows == ids, 1.0, 0.0).astype(jnp.bfloat16)
-        both = jnp.concatenate(split2(data), axis=1)
-        part = dot32(chooser, both)
-        if s == 0:
-            acc[...] = part
-        else:
-            acc[...] += part
-    sums[...] = acc[:, :BLK] + acc[:, BLK:]
+        lambda got_ref, out_ref: sum_side(side, got_ref, out_ref),
+        out_shape=jax.ShapeDtypeStruct((LEV * TILES, BLK), jnp.float32),
+        compiler_params=pltpu.CompilerParams(vmem_limit_bytes=24 << 20),
+        cost_estimate=pl.CostEstimate(flops=100_000_000, bytes_accessed=1_000_000, transcendentals=0),
+        interpret=interpret,
+        name=("core", "own", "chip")[side],
+    )(got)
+
+
+def by_row_kernel(own_ref, core_ref, chip_ref, out_ref, sums):
+    sums[...] = own_ref[...] + core_ref[...] + chip_ref[...]
     lane = lax.broadcasted_iota(jnp.int32, (LEV, BLK), 1)
     for lat in range(LATB):
         for half in range(2):
@@ -186,19 +164,16 @@
             out_ref[lat // 2, at : at + LEV, :] = value
 
 
-def combine(reg, irr, interpret=False):
+def by_row(own, core, chip, interpret=False):
     return pl.pallas_call(
-        combine_kernel,
+        by_row_kernel,
         out_shape=jax.ShapeDtypeStruct((COLS, P2_ROWS, BLK), jnp.float32),
-        scratch_shapes=[
-            pltpu.VMEM((LEV * TILES, 2 * BLK), jnp.float32),
-            pltpu.VMEM((LEV * TILES, BLK), jnp.float32),
-        ],
-        compiler_params=pltpu.CompilerParams(vmem_limit_bytes=24 << 20),
-        cost_estimate=pl.CostEstimate(flops=1_600_000_000, bytes_accessed=2_000_000, transcendentals=0),
-        interpret=interpret,
-        name="combine",
-    )(reg, irr)
+        scratch_shapes=[pltpu.VMEM((LEV * TILES, BLK), jnp.float32)],
+        compiler_params=pltpu.CompilerParams(vmem_limit_bytes=12 << 20),
+        cost_estimate=pl.CostEstimate(flops=1_000_000, bytes_accessed=1_500_000, transcendentals=0),
+        interpret=interpret,
+        name="by_row",
+    )(own, core, chip)
 
 
 def filter_kernel(cut_ref, x_ref, f_ref, ft_ref, g_ref, gt_ref, tc_ref, ts_ref, out_ref):
@@ -311,13 +286,11 @@
 
 def local(source, weights, source_block, owner_device, target_tile, cutoff):
     bands = lax.axis_size("band")
-    reg, own, up, down = place(source, weights, source_block, owner_device[:, 0], target_tile)
-    steps = [(i, i + 1) for i in range(bands - 1)]
-    below = lax.ppermute(up, "band", steps)
-    above = lax.ppermute(down, "band", [(j, i) for i, j in steps])
-    reg = exchange(reg)
-    irr = exchange(join(own, below, above))
-    rows = combine(reg, irr)
+    got = exchange(place(source, weights, source_block, owner_device[:, 0], target_tile))
+    got = got.reshape(COLS * ROWS, BLK)
+    chip = lax.ppermute(tile_sums(got, 2), "band", [(i, i + 1 if i % 2 else i - 1) for i in range(1, bands - 1)])
+    core = lax.ppermute(tile_sums(got, 0), "band", [(i, i ^ 1) for i in range(bands)])
+    rows = by_row(tile_sums(got, 1), core, chip)
     remapped = by_latitude(rows)
     rows = exchange(rows)
     rows = zonal_filter(rows, cutoff, zonal_tables())

time: 130 us -> 120 us (0.923)
  starting transfers between devices: 36.6 us -> 23.9 us
  waiting for transfers between devices: 73.3 us -> 78.5 us
  Pallas kernels: 17.1 us -> 15.8 us
    all_to_all x4 -> x3, starting transfers between devices: 31 us -> 21.4 us  [exchange(): return lax.all_to_all(array, 'col', 0, 0, tiled=True)]
    all_to_all x4 -> x3, waiting for transfers between devices: 64.9 us -> 72.7 us  [exchange(): return lax.all_to_all(array, 'col', 0, 0, tiled=True)]
    ppermute x2, starting transfers between devices: 5.56 us -> 2.54 us  [the longest x1 2.45 us: local(): lax.ppermute(tile_sums(got, 2), 'band', [(i, i + 1 if i % 2 else i - 1) f...]
    ppermute x2, waiting for transfers between devices: 8.4 us -> 5.76 us  [the longest x1 5.76 us: local(): lax.ppermute(tile_sums(got, 2), 'band', [(i, i + 1 if i % 2 else i - 1) f...]
    pallas_call x3 -> x5, Pallas kernels: 11.1 us -> 9.72 us  [the longest x1 7.05 us: place(): pl.pallas_call(place_kernel, out_shape=jax.ShapeDtypeStruct((COLS, ROWS,...]
  transfers between devices with their start and end apart: 6 -> 5, of which waited for: 5 -> 4; matrix products, arithmetic and copies ran while one was open for 1% -> 1% of each run, Pallas kernels for 2% -> 2%
where the time goes in v2:
time: 120 us
  waiting for transfers between devices  78.5 us (65%)
  starting transfers between devices  23.9 us (20%)
  Pallas kernels  15.8 us (13%)
    all_to_all x3, waiting for transfers between devices, exchange(): return lax.all_to_all(array, 'col', 0, 0, tiled=True)  72.7 us
    all_to_all x3, starting transfers between devices, exchange(): return lax.all_to_all(array, 'col', 0, 0, tiled=True)  21.4 us
    pallas_call x1, Pallas kernels, place(): pl.pallas_call(place_kernel, out_shape=jax.ShapeDtypeStruct((COLS, ROWS,...  7.05 us
    ppermute x1, waiting for transfers between devices, local(): lax.ppermute(tile_sums(got, 2), 'band', [(i, i + 1 if i % 2 else i - 1) f...  5.76 us
    pallas_call x1, Pallas kernels, zonal_filter(): pl.pallas_call(filter_kernel, out_shape=jax.ShapeDtypeStruct((COLS * P2_R...  3.35 us
    pallas_call x2, Pallas kernels, by_latitude(): pl.pallas_call(lay_kernel, out_shape=jax.ShapeDtypeStruct((LEV, LATB, LON...  2.69 us
    ppermute x1, starting transfers between devices, local(): lax.ppermute(tile_sums(got, 2), 'band', [(i, i + 1 if i % 2 else i - 1) f...  2.45 us
  transfers between devices with their start and end apart: 5, of which 4 were waited for; matrix products, arithmetic and copies ran while one was open for 1% of the time, Pallas kernels for 2%

profile of v2, /device:TPU:8, one launch (start us, length us, event | category | flops | bytes accessed | tf_op | source)
XLA Modules:
  0.0 119.9 jit_solution(13864823203969120240)
XLA Ops:
  0.6 7.1 %place.1 = f32[32,112,128]{2,1,0:T(8,128)} custom-call(s32[256]{0:T(256)} %sb_hbm.1, s32[256]{0:T(256)} %bitcast.43, s32[256]{0:T(256)} %tile_hbm.1, bf16[6,16384]{1,0:T(8,128)(2,1)} %src_hbm.1, bf16[256,128,128]{2,1,0:T(8,128)(2,1)} %w_hbm.1), custom_call_target="tpu_custom_call" | custom-call | flops 100000000 | bytes 10000000 | tf_op jit(solution)/shard_map/place/pallas_call | solution.py:101
  7.7 11.3 %all-to-all-start = ((f32[32,112,128]{2,1,0:T(8,128)}), f32[32,112,128]{2,1,0:T(8,128)S(1)}, u32[]{:S(2)}, u32[]{:S(2)}) async-start(f32[32,112,128]{2,1,0:T(8,128)} %place.1), calls=%async_computation | async-start | bytes 3670016 | tf_op jit(solution)/shard_map/all_to_all | solution.py:284
  19.0 0.1 fusion.27
  19.1 0.1 reduce-precision_convert_fusion.3
  19.2 0.1 copy.8.f_ref
  19.3 44.3 %all-to-all-done = f32[32,112,128]{2,1,0:T(8,128)S(1)} async-done(((f32[32,112,128]{2,1,0:T(8,128)}), f32[32,112,128]{2,1,0:T(8,128)S(1)}, u32[]{:S(2)}, u32[]{:S(2)}) %all-to-all-start) | async-done | bytes 1835040 | tf_op jit(solution)/shard_map/all_to_all | solution.py:284
  63.7 1.0 core.1
  64.7 0.3 chip.1
  65.0 0.1 collective-permute-start
  65.1 2.4 %collective-permute-start.1 = (f32[720,128]{1,0:T(8,128)S(1)}, f32[720,128]{1,0:T(8,128)S(1)}, u32[]{:S(2)}, u32[]{:S(2)}) collective-permute-start(f32[720,128]{1,0:T(8,128)S(1)} %chip.1), channel_id=1, source_target_pairs={{32,64},{64,32},{96,128},{128,96},{160,192},{192,160},{33,65},{65,... | collective-permute-start | bytes 1105928 | tf_op jit(solution)/shard_map/ppermute | solution.py:291
  67.5 0.1 sine_select_fusion
  67.6 0.2 copy.9.g_ref
  67.8 0.3 own.1.own_ref
  68.1 0.0 copy-start
  68.1 0.0 collective-permute-done.core_ref
  68.1 5.8 %collective-permute-done.1.chip_ref = f32[720,128]{1,0:T(8,128)S(1)} collective-permute-done((f32[720,128]{1,0:T(8,128)S(1)}, f32[720,128]{1,0:T(8,128)S(1)}, u32[]{:S(2)}, u32[]{:S(2)}) %collective-permute-start.1) | collective-permute-done | bytes 368672 | tf_op jit(solution)/shard_map/ppermute | solution.py:291
  73.9 1.1 by_row.1
  75.0 5.9 %all-to-all-start.1 = ((f32[32,24,128]{2,1,0:T(8,128)}), f32[32,24,128]{2,1,0:T(8,128)S(1)}, u32[]{:S(2)}, u32[]{:S(2)}) async-start(f32[32,24,128]{2,1,0:T(8,128)} %by_row.1), calls=%async_computation.1 | async-start | bytes 786432 | tf_op jit(solution)/shard_map/all_to_all | solution.py:284
  80.8 0.1 sine_negate_fusion
  80.9 0.1 fusion.25
  81.0 0.2 fusion.7
  81.2 15.6 %all-to-all-done.1 = f32[32,24,128]{2,1,0:T(8,128)S(1)} async-done(((f32[32,24,128]{2,1,0:T(8,128)}), f32[32,24,128]{2,1,0:T(8,128)S(1)}, u32[]{:S(2)}, u32[]{:S(2)}) %all-to-all-start.1) | async-done | bytes 393248 | tf_op jit(solution)/shard_map/all_to_all | solution.py:284
  96.9 0.0 copy-done
  96.9 3.3 %zonal.1 = f32[768,128]{1,0:T(8,128)} custom-call(s32[2]{0:T(128)S(1)} %copy-done, f32[768,128]{1,0:T(8,128)S(1)} %bitcast.42, bf16[2,64,32]{2,1,0:T(8,128)(2,1)S(1)} %copy.8.f_ref, bf16[2,32,64]{2,1,0:T(8,128)(2,1)S(1)} %pad_maximum_fusion.5.ft_ref, bf16[2,512,32]{2,1,0:T(8,128)(2,1)S(1)} %copy.9.g_ref, bf16[2,32,512]{2,1,0:T(8,128)(2,1)S(1)} %pad_maximum_fusion.2.gt_ref, ...), custom_call_target="tpu_custom_call" | custom-call | flops 300000000 | bytes 1000000 | tf_op jit(solution)/shard_map/zonal/pallas_call | solution.py:223
  100.2 4.2 %all-to-all-start.2 = ((f32[32,24,128]{2,1,0:T(8,128)}), f32[32,24,128]{2,1,0:T(8,128)S(1)}, u32[]{:S(2)}, u32[]{:S(2)}) async-start(f32[32,24,128]{2,1,0:T(8,128)} %bitcast.14), calls=%async_computation.2 | async-start | bytes 786432 | tf_op jit(solution)/shard_map/all_to_all | solution.py:284
  104.4 1.8 %lay.2 = f32[6,64,225]{2,1,0:T(8,128)} custom-call(f32[768,128]{1,0:T(8,128)} %bitcast.2.rows_ref), custom_call_target="tpu_custom_call" | custom-call | flops 1000000 | bytes 800000 | tf_op jit(solution)/shard_map/lay/pallas_call | solution.py:272
  106.3 12.8 %all-to-all-done.2 = f32[32,24,128]{2,1,0:T(8,128)S(1)} async-done(((f32[32,24,128]{2,1,0:T(8,128)}), f32[32,24,128]{2,1,0:T(8,128)S(1)}, u32[]{:S(2)}, u32[]{:S(2)}) %all-to-all-start.2) | async-done | bytes 393248 | tf_op jit(solution)/shard_map/all_to_all | solution.py:284
  119.0 0.8 lay.3
  (8 shorter events, 0.1 us)
Async XLA Ops:
  7.7 56.0 %all-to-all-start = ((f32[32,112,128]{2,1,0:T(8,128)}), f32[32,112,128]{2,1,0:T(8,128)S(1)}, u32[]{:S(2)}, u32[]{:S(2)}) async-start(f32[32,112,128]{2,1,0:T(8,128)} %place.1), calls=%async_computation | async-start | bytes 3670016 | tf_op jit(solution)/shard_map/all_to_all | solution.py:284
  65.0 3.2 %collective-permute-start = (f32[720,128]{1,0:T(8,128)}, f32[720,128]{1,0:T(8,128)S(1)}, u32[]{:S(2)}, u32[]{:S(2)}) collective-permute-start(f32[720,128]{1,0:T(8,128)} %core.1), channel_id=1, source_target_pairs={{0,32},{32,0},{64,96},{96,64},{128,160},{160,128},{192,224},{224,1... | collective-permute-start | bytes 1105928 | tf_op jit(solution)/shard_map/ppermute | solution.py:292
  65.1 8.8 %collective-permute-start.1 = (f32[720,128]{1,0:T(8,128)S(1)}, f32[720,128]{1,0:T(8,128)S(1)}, u32[]{:S(2)}, u32[]{:S(2)}) collective-permute-start(f32[720,128]{1,0:T(8,128)S(1)} %chip.1), channel_id=1, source_target_pairs={{32,64},{64,32},{96,128},{128,96},{160,192},{192,160},{33,65},{65,... | collective-permute-start | bytes 1105928 | tf_op jit(solution)/shard_map/ppermute | solution.py:291
  68.1 28.8 %copy-start = (s32[2]{0:T(128)S(1)}, s32[2]{0:T(128)}, u32[]{:S(2)}) copy-start(s32[2]{0:T(128)} %cut_ref.1) | copy-start | bytes 28
  75.0 21.9 %all-to-all-start.1 = ((f32[32,24,128]{2,1,0:T(8,128)}), f32[32,24,128]{2,1,0:T(8,128)S(1)}, u32[]{:S(2)}, u32[]{:S(2)}) async-start(f32[32,24,128]{2,1,0:T(8,128)} %by_row.1), calls=%async_computation.1 | async-start | bytes 786432 | tf_op jit(solution)/shard_map/all_to_all | solution.py:284
  100.2 18.8 %all-to-all-start.2 = ((f32[32,24,128]{2,1,0:T(8,128)}), f32[32,24,128]{2,1,0:T(8,128)S(1)}, u32[]{:S(2)}, u32[]{:S(2)}) async-start(f32[32,24,128]{2,1,0:T(8,128)} %bitcast.14), calls=%async_computation.2 | async-start | bytes 786432 | tf_op jit(solution)/shard_map/all_to_all | solution.py:284
